TPU v7x, 128 devices: a whole 4x4x4 slice. The times are simulated.
128 devices in a mesh: bank: 4 (over y), zero: 32 (over z, x, core).
Axes of the slice: x: 4, y: 4, z: 4, core: 2. Of those that a mesh axis runs over, the one named last changes fastest.
Arguments:
- train_gate: float32 [64, 2048, 1024], P('bank', 'zero'), may hold values from -0.25 to 0.25
- train_up: float32 [64, 2048, 1024], P('bank', 'zero'), may hold values from -0.25 to 0.25
- train_down: float32 [64, 1024, 2048], P('bank', None, 'zero'), may hold values from -0.375 to 0.375
- router_weight: float32 [2048, 64], P('zero', 'bank'), may hold values from -0.125 to 0.125
- router_gain: float32 [2048], P('zero'), may hold values from 0.25 to 1.75
Outputs:
- ready_gate: bfloat16 [64, 2048, 1024], P('bank', None, 'zero')
- ready_up: bfloat16 [64, 2048, 1024], P('bank', None, 'zero')
- ready_down: bfloat16 [64, 1024, 2048], P('bank', 'zero')
- scale_gate: float32 [64, 1024], P('bank', 'zero')
- scale_up: float32 [64, 1024], P('bank', 'zero')
- scale_down: float32 [64, 1024], P('bank', 'zero')
- serve_router: bfloat16 [2048, 64], replicated
All inputs are finite; a program needn't handle non-finite values.
Results may differ from a plain program's by a relative error of at most 0.001.
Values may be sent and summed in bfloat16 or wider, within the bound.
A program may use at most 128 MiB of HBM per device.

v0:
```python
import jax
import jax.numpy as jnp
from jax import lax
from jax.sharding import Mesh
from jax.sharding import PartitionSpec as P

ZERO = ("zero_0", "zero_1", "zero_2")


def packed_total(arrays, axis):
    ends = [0]
    for a in arrays:
        ends.append(ends[-1] + a.size)
    total = lax.psum(jnp.concatenate([a.ravel() for a in arrays]), axis)
    return tuple(total[b:e].reshape(a.shape) for a, b, e in zip(arrays, ends, ends[1:]))


def laid_out(pieces, dim):
    lengths = list(pieces.shape[1:])
    lengths[dim] *= pieces.shape[0]
    return jnp.moveaxis(pieces, 0, dim).reshape(lengths)


def all_blocks(value, axes, turns):
    pieces = value[None]
    for k in turns:
        pieces = lax.all_gather(pieces, axes[k], axis=0, tiled=True)
    current = [lax.axis_size(axes[k]) for k in reversed(turns)]
    pieces = pieces.reshape(*current, *value.shape)
    turned = sorted(range(len(turns)), key=lambda place: turns[len(turns) - 1 - place])
    return pieces.transpose(*turned, *range(len(turns), pieces.ndim)).reshape(-1, *value.shape)


def gather_axes(value, axes, turns, dim):
    return laid_out(all_blocks(value, axes, turns), dim)


def body(train_gate, train_up, train_down, router_weight, router_gain):
    total_gate, total_up, total_down = packed_total(
        (
            jnp.sum(train_gate * train_gate, axis=1),
            jnp.sum(train_up * train_up, axis=1),
            jnp.sum(train_down * train_down, axis=2),
        ),
        ZERO,
    )
    scale_gate = jnp.sqrt(total_gate)
    scale_up = jnp.sqrt(total_up)
    scale_down = jnp.sqrt(total_down)
    narrow_gate, narrow_up, narrow_down = (
        (train_gate / jnp.expand_dims(scale_gate, 1)).astype(jnp.bfloat16),
        (train_up / jnp.expand_dims(scale_up, 1)).astype(jnp.bfloat16),
        (train_down / jnp.expand_dims(scale_down, 2)).astype(jnp.bfloat16),
    )
    ready_gate, ready_up = (
        lax.all_to_all(narrow_gate, ZERO, split_axis=2, concat_axis=1, tiled=True),
        lax.all_to_all(narrow_up, ZERO, split_axis=2, concat_axis=1, tiled=True),
    )
    ready_down = lax.all_to_all(narrow_down, ZERO, split_axis=1, concat_axis=2, tiled=True)
    scale_gate = lax.dynamic_slice_in_dim(
        scale_gate, lax.axis_index(ZERO) * ready_gate.shape[2], ready_gate.shape[2], axis=1
    )
    scale_up = lax.dynamic_slice_in_dim(
        scale_up, lax.axis_index(ZERO) * ready_up.shape[2], ready_up.shape[2], axis=1
    )
    scale_down = lax.dynamic_slice_in_dim(
        scale_down, lax.axis_index(ZERO) * ready_down.shape[1], ready_down.shape[1], axis=1
    )
    part_router = (router_weight * router_gain[:, None]).astype(jnp.bfloat16)
    row_router = gather_axes(part_router, (("zero_0", "zero_1"), "zero_2"), (0, 1), 0)
    serve_router = lax.all_gather(row_router, "bank", axis=1, tiled=True)
    return (ready_gate, ready_up, ready_down, scale_gate, scale_up, scale_down, serve_router)


def solution(mesh):
    split = Mesh(
        mesh.devices.reshape(mesh.shape["bank"], 4, 4, 2), ("bank", "zero_0", "zero_1", "zero_2")
    )
    placed = (
        P("bank", ZERO, None),
        P("bank", ZERO, None),
        P("bank", None, ZERO),
        P(ZERO, "bank"),
        P(ZERO),
    )
    return jax.shard_map(
        body,
        mesh=split,
        in_specs=placed,
        out_specs=(
            P("bank", None, ZERO),
            P("bank", None, ZERO),
            P("bank", ZERO, None),
            P("bank", ZERO),
            P("bank", ZERO),
            P("bank", ZERO),
            P(),
        ),
        check_vma=False,
    )
```

profile of v0, /device:TPU:1, one launch (start us, length us, event | category | flops | bytes accessed | tf_op | source)
XLA Modules:
  0.0 337.6 jit_solution(13221425438647020591)
XLA Ops:
  13.3 8.1 %copy.28 = f32[16,64,1024]{1,0,2:T(8,128)} copy(f32[16,64,1024]{2,1,0:T(8,128)} %param.5) | data formatting | bytes 8388608 | tf_op args[0]
  21.4 98.1 %all-reduce.2.cloned.1.call-done = f32[49152]{0:T(1024)} async-done(((f32[49152]{0:T(1024)}), f32[49152]{0:T(1024)}) %all-reduce.2.cloned.1.call-update) | async-done | bytes 196624 | tf_op jit(solution)/shard_map/psum | solution.py:14
  120.7 6.9 %fusion.1 = bf16[1024,16,64]{2,1,0:T(8,128)(2,1)} fusion(f32[16,64,1024]{1,0,2:T(8,128)} %copy.28, f32[16,1024]{0,1:T(8,128)S(1)} %copy.27), kind=kLoop, calls=%fused_computation.15 | loop fusion | flops 2097152 | bytes 6356992
  127.5 7.9 %reshape.68 = bf16[32,2,16384]{2,1,0:T(2,128)(2,1)} reshape(bf16[1024,16,64]{2,1,0:T(8,128)(2,1)} %fusion.1) | data formatting | bytes 4194304
  141.0 8.1 %copy.32 = f32[16,64,1024]{1,0,2:T(8,128)} copy(f32[16,64,1024]{2,1,0:T(8,128)} %param.6) | data formatting | bytes 8388608 | tf_op args[1]
  149.3 6.9 %fusion.2 = bf16[1024,16,64]{2,1,0:T(8,128)(2,1)} fusion(f32[16,64,1024]{1,0,2:T(8,128)} %copy.32, f32[16,1024]{0,1:T(8,128)S(1)} %copy.31), kind=kLoop, calls=%fused_computation.16 | loop fusion | flops 2097152 | bytes 6356992
  156.2 7.9 %reshape.70 = bf16[32,2,16384]{2,1,0:T(2,128)(2,1)} reshape(bf16[1024,16,64]{2,1,0:T(8,128)(2,1)} %fusion.2) | data formatting | bytes 4194304
  164.1 6.1 %all-to-all-done = bf16[32,2,16384]{2,1,0:T(2,128)(2,1)S(1)} async-done(((bf16[32,2,16384]{2,1,0:T(2,128)(2,1)}), bf16[32,2,16384]{2,1,0:T(2,128)(2,1)S(1)}, u32[]{:S(2)}, u32[]{:S(2)}) %all-to-all-start) | async-done | bytes 2097184 | tf_op jit(solution)/shard_map/all_to_all | solution.py:56
  175.4 8.1 %copy.36 = f32[16,1024,64]{2,0,1:T(8,128)} copy(f32[16,1024,64]{1,2,0:T(8,128)} %param.7) | data formatting | bytes 8388608 | tf_op args[2]
  183.7 6.9 %fusion.3 = bf16[1024,16,64]{2,1,0:T(8,128)(2,1)} fusion(f32[16,1024,64]{2,0,1:T(8,128)} %copy.36, f32[16,1024]{0,1:T(8,128)S(1)} %copy.35), kind=kLoop, calls=%fused_computation.17 | loop fusion | flops 2097152 | bytes 6356992
  190.5 7.9 %reshape.72 = bf16[32,2,16384]{2,1,0:T(2,128)(2,1)} reshape(bf16[1024,16,64]{2,1,0:T(8,128)(2,1)} %fusion.3) | data formatting | bytes 4194304
  198.4 5.8 %all-to-all-done.1 = bf16[32,2,16384]{2,1,0:T(2,128)(2,1)} async-done(((bf16[32,2,16384]{2,1,0:T(2,128)(2,1)}), bf16[32,2,16384]{2,1,0:T(2,128)(2,1)}, u32[]{:S(2)}, u32[]{:S(2)}) %all-to-all-start.1) | async-done | bytes 2097184 | tf_op jit(solution)/shard_map/all_to_all | solution.py:57
  204.2 6.5 %all-to-all-start.2 = ((bf16[32,2,16384]{2,1,0:T(2,128)(2,1)}), bf16[32,2,16384]{2,1,0:T(2,128)(2,1)}, u32[]{:S(2)}, u32[]{:S(2)}) async-start(bf16[32,2,16384]{2,1,0:T(2,128)(2,1)} %reshape.72), calls=%async_computation.2 | async-start | bytes 4194304 | tf_op jit(solution)/shard_map/all_to_all | solution.py:59
  210.7 40.2 %all-gather.1 = bf16[16,64,16]{1,2,0:T(8,128)(2,1)S(1)} all-gather(bf16[1,64,16]{1,2,0:T(8,128)(2,1)S(1)} %fusion), channel_id=2, replica_groups=mesh['bank'=4,'zero_0'=4,'zero_1'=4,'zero_2'=2] {'zero_0','zero_1'}, dimensions={0}, use_global_device_ids=true | all-gather | bytes 34816 | tf_op jit(solution)/shard_map/all_gather | solution.py:27
  250.9 6.5 %all_gather.10 = bf16[32,64,16]{1,2,0:T(8,128)(2,1)S(1)} all-gather(bf16[16,64,16]{1,2,0:T(8,128)(2,1)S(1)} %all-gather.1), channel_id=1, replica_groups=mesh['bank'=4,'zero_0'=4,'zero_1'=4,'zero_2'=2] {'zero_2'}, dimensions={0}, use_global_device_ids=true | all-gather | bytes 98304 | tf_op jit(solution)/shard_map/all_gather | solution.py:27
  257.8 10.3 %all_gather.11 = bf16[2048,64]{0,1:T(8,128)(2,1)S(1)} all-gather(bf16[2048,16]{0,1:T(8,128)(2,1)S(1)} %reshape_reshape.3), channel_id=1, replica_groups=mesh['bank'=4,'zero_0'=4,'zero_1'=4,'zero_2'=2] {'bank'}, dimensions={1}, use_global_device_ids=true | all-gather | bytes 327680 | tf_op jit(solution)/shard_map/all_gather | solution.py:71
  273.4 6.9 %copy.30 = bf16[16,32,64,32]{2,1,3,0:T(8,128)(2,1)} copy(bf16[16,32,64,32]{2,0,3,1:T(8,128)(2,1)} %bitcast.41) | data formatting | bytes 4194304 | tf_op jit(solution)/shard_map/all_to_all | solution.py:56
  280.2 6.7 %all_to_all.42 = bf16[16,2048,32]{1,2,0:T(8,128)(2,1)} reshape(bf16[16,32,64,32]{2,1,3,0:T(8,128)(2,1)} %copy.30) | data formatting | bytes 4194304 | tf_op jit(solution)/shard_map/all_to_all | solution.py:56
  287.0 7.9 %reshape.71 = bf16[1024,16,64]{2,1,0:T(8,128)(2,1)} reshape(bf16[32,2,16384]{2,1,0:T(2,128)(2,1)} %all-to-all-done.1) | data formatting | bytes 4194304
  294.9 6.9 %copy.34 = bf16[16,32,64,32]{2,1,3,0:T(8,128)(2,1)} copy(bf16[16,32,64,32]{2,0,3,1:T(8,128)(2,1)} %bitcast.42) | data formatting | bytes 4194304 | tf_op jit(solution)/shard_map/all_to_all | solution.py:57
  301.8 6.7 %all_to_all.46 = bf16[16,2048,32]{1,2,0:T(8,128)(2,1)} reshape(bf16[16,32,64,32]{2,1,3,0:T(8,128)(2,1)} %copy.34) | data formatting | bytes 4194304 | tf_op jit(solution)/shard_map/all_to_all | solution.py:57
  308.5 7.9 %reshape.73 = bf16[1024,16,64]{2,1,0:T(8,128)(2,1)} reshape(bf16[32,2,16384]{2,1,0:T(2,128)(2,1)} %all-to-all-done.2) | data formatting | bytes 4194304
  316.5 6.9 %copy.38 = bf16[16,32,32,64]{3,2,1,0:T(8,128)(2,1)} copy(bf16[16,32,32,64]{3,0,1,2:T(8,128)(2,1)} %bitcast.43) | data formatting | bytes 4194304 | tf_op jit(solution)/shard_map/all_to_all | solution.py:59
  323.3 6.7 %all_to_all.50 = bf16[16,32,2048]{2,1,0:T(8,128)(2,1)} reshape(bf16[16,32,32,64]{3,2,1,0:T(8,128)(2,1)} %copy.38) | data formatting | bytes 4194304 | tf_op jit(solution)/shard_map/all_to_all | solution.py:59
  (34 shorter events, 24.8 us)
Async XLA Ops:
  7.2 112.3 %all-reduce.2.cloned.1.call-start = ((), (), s32[]{:S(2)}) async-start(), calls=%async_computation.3 | async-start | bytes 393216 | tf_op jit(solution)/shard_map/psum | solution.py:14
  7.2 3.5 %copy-start = (f32[16,64,1024]{2,1,0:T(8,128)S(1)}, f32[16,64,1024]{2,1,0:T(8,128)}, u32[]{:S(2)}) copy-start(f32[16,64,1024]{2,1,0:T(8,128)} %param.6) | copy-start | bytes 12582916
  7.2 4.7 %copy-start.1 = (f32[16,1024,64]{1,2,0:T(8,128)S(1)}, f32[16,1024,64]{1,2,0:T(8,128)}, u32[]{:S(2)}) copy-start(f32[16,1024,64]{1,2,0:T(8,128)} %param.7) | copy-start | bytes 12582916
  135.4 34.7 %all-to-all-start = ((bf16[32,2,16384]{2,1,0:T(2,128)(2,1)}), bf16[32,2,16384]{2,1,0:T(2,128)(2,1)S(1)}, u32[]{:S(2)}, u32[]{:S(2)}) async-start(bf16[32,2,16384]{2,1,0:T(2,128)(2,1)} %reshape.68), calls=%async_computation | async-start | bytes 4194304 | tf_op jit(solution)/shard_map/all_to_all | solution.py:56
  170.1 34.1 %all-to-all-start.1 = ((bf16[32,2,16384]{2,1,0:T(2,128)(2,1)}), bf16[32,2,16384]{2,1,0:T(2,128)(2,1)}, u32[]{:S(2)}, u32[]{:S(2)}) async-start(bf16[32,2,16384]{2,1,0:T(2,128)(2,1)} %reshape.70), calls=%async_computation.1 | async-start | bytes 4194304 | tf_op jit(solution)/shard_map/all_to_all | solution.py:57
  190.5 20.1 %copy-start.2 = (f32[64,16]{0,1:T(8,128)S(1)}, f32[64,16]{0,1:T(8,128)}, u32[]{:S(2)}) copy-start(f32[64,16]{0,1:T(8,128)} %param.8) | copy-start | bytes 12292
  190.5 20.1 %copy-start.3 = (f32[64]{0:T(128)S(1)}, f32[64]{0:T(128)}, u32[]{:S(2)}) copy-start(f32[64]{0:T(128)} %param.9) | copy-start | bytes 772
  204.2 104.4 %all-to-all-start.2 = ((bf16[32,2,16384]{2,1,0:T(2,128)(2,1)}), bf16[32,2,16384]{2,1,0:T(2,128)(2,1)}, u32[]{:S(2)}, u32[]{:S(2)}) async-start(bf16[32,2,16384]{2,1,0:T(2,128)(2,1)} %reshape.72), calls=%async_computation.2 | async-start | bytes 4194304 | tf_op jit(solution)/shard_map/all_to_all | solution.py:59
Sparse Core Ops, SparseCore 0:
  13.4 106.0 all-reduce.1
where the time goes:
time: 341 us; the launch traced here: 338 us
  local copies, waits for them, and re-layouts  114 us (33%)
  waiting for transfers between devices  110 us (32%)
  blocking collectives  57 us (17%)
  other arithmetic  25.5 us (7%)
  starting transfers between devices  17.3 us (5%)
  between operations  14.2 us (4%)
    psum x1, waiting for transfers between devices, packed_total(): total = lax.psum(jnp.concatenate([a.ravel() for a in arrays]), axis)  98.1 us
    unnamed x21, local copies, waits for them, and re-layouts  69.7 us
    all_gather x2, blocking collectives, all_blocks(): pieces = lax.all_gather(pieces, axes[k], axis=0, tiled=True)  46.8 us
    unnamed x4, other arithmetic  20.6 us
    all_to_all x2, local copies, waits for them, and re-layouts, body(): lax.all_to_all(narrow_down, ZERO, split_axis=1, concat_axis=2, tiled=True)  13.6 us
    all_to_all x2, local copies, waits for them, and re-layouts, body(): lax.all_to_all(narrow_gate, ZERO, split_axis=2, concat_axis=1, tiled=True)  13.6 us
    all_to_all x2, local copies, waits for them, and re-layouts, body(): lax.all_to_all(narrow_up, ZERO, split_axis=2, concat_axis=1, tiled=True)  13.6 us
    all_gather x1, blocking collectives, body(): serve_router = lax.all_gather(row_router, 'bank', axis=1, tiled=True)  10.3 us
  transfers between devices with their start and end apart: 4, of which 3 were waited for; matrix products, arithmetic and copies ran while one was open for 24% of the time, Pallas kernels for 0%

commit v1 on v0

v1 whole, which is shorter than its diff:
```python
import functools

import jax
import jax.numpy as jnp
from jax import lax
from jax.experimental import pallas as pl
from jax.experimental.pallas import tpu as pltpu
from jax.sharding import Mesh
from jax.sharding import PartitionSpec as P

ZERO = ("z", "x", "c")
MESH = pl.DeviceIdType.MESH
F32 = jnp.float32
BF16 = jnp.bfloat16
HALF = 8
SLOTS = 3 * HALF
PAIRS = SLOTS // 2
LAG = 2
GROUPS = ((0, 2), (2, 6), (8, 8), (16, 8))


def kernel(
    gate, up, down, weight, gain, out, scales, router,
    full, turned, relay, xsum, zsum, scale, other, inverse, swap, part,
    load_sem, core_send, core_recv, xs_send, xs_recv, zs_send, zs_recv,
    one_send, one_recv, two_send, two_recv, sc_send, sc_recv, rt_send, rt_recv,
):
    b, z, x, c = (lax.axis_index(n) for n in ("b", "z", "x", "c"))
    oc = 1 - c

    def xdev(k):
        return {"x": lax.rem(x + k, 4)}

    def zdev(k):
        return {"z": lax.rem(z + k, 4)}

    def remote(src, dst, send, recv, dev):
        pltpu.make_async_remote_copy(
            src_ref=src, dst_ref=dst, send_sem=send, recv_sem=recv, device_id=dev, device_id_type=MESH
        ).start()

    def wait_bytes(ref, sem):
        pltpu.make_async_copy(ref, ref, sem).wait()

    sources = (gate, up, down)
    mine = pl.ds(pl.multiple_of(c * 64, 64), 64)

    for k, (first, n) in enumerate(GROUPS):
        src = sources[first // HALF]
        pltpu.make_async_copy(
            src.at[pl.ds(c * HALF + first % HALF, n)], full.at[pl.ds(first, n), mine], load_sem.at[k]
        ).start()

    barrier = pltpu.get_barrier_semaphore()
    peers = [{"c": oc}]
    for k in (1, 2, 3):
        peers += [xdev(k), zdev(k), {**xdev(k), "c": oc}, {**zdev(k), "c": oc}, {"b": lax.rem(b + k, 4)}]
    for dev in peers:
        pl.semaphore_signal(barrier, inc=1, device_id=dev, device_id_type=MESH)

    product = weight[...] * gain[...]
    swap[0] = jnp.concatenate([product, product], axis=1).reshape(2, HALF, 128)
    pl.semaphore_wait(barrier, len(peers))

    for k, (first, n) in enumerate(GROUPS):
        src = sources[first // HALF]
        remote(
            src.at[pl.ds(oc * HALF + first % HALF, n)], full.at[pl.ds(first, n), mine],
            core_send.at[k], core_recv.at[k], {"c": oc},
        )
    remote(swap.at[0, oc], swap.at[1, 0], rt_send.at[0], rt_recv.at[0], {"c": oc})

    def sums(k):
        first, n = GROUPS[k]
        pltpu.make_async_copy(
            gate.at[pl.ds(0, n)], full.at[pl.ds(first, n), mine], load_sem.at[k]
        ).wait()
        wait_bytes(full.at[pl.ds(first, n), mine], core_recv.at[k])

        def one(q, carry):
            rows = full[q]
            xsum[x, q] = jnp.sum(rows * rows, axis=0, keepdims=True)
            return carry

        lax.fori_loop(first, first + n, one, 0)
        at = pl.ds(first, n)
        for j in (1, 2, 3):
            remote(xsum.at[x, at], xsum.at[x, at], xs_send.at[k], xs_recv.at[k], xdev(j))

    def fold_x(k):
        first, n = GROUPS[k]
        at = pl.ds(first, n)
        wait_bytes(xsum.at[pl.ds(0, 3), at], xs_recv.at[k])
        zsum[z, at] = (xsum[0, at] + xsum[1, at]) + (xsum[2, at] + xsum[3, at])
        for j in (1, 2, 3):
            remote(zsum.at[z, at], zsum.at[z, at], zs_send.at[k], zs_recv.at[k], zdev(j))

    def fold_z(k):
        first, n = GROUPS[k]
        at = pl.ds(first, n)
        wait_bytes(zsum.at[pl.ds(0, 3), at], zs_recv.at[k])
        root = jnp.sqrt((zsum[0, at] + zsum[1, at]) + (zsum[2, at] + zsum[3, at]))
        scale[at] = root
        inverse[at] = 1.0 / root

    def turn(q):
        for j in range(8):
            lanes = slice(j * 128, (j + 1) * 128)
            block = (full[q, :, lanes] * inverse[q, :, lanes]).astype(BF16)
            turned[q, j // 2, (j % 2) * 2 : (j % 2) * 2 + 2] = block.T.reshape(2, 64, 128)

    xlane = pl.ds(pl.multiple_of(x * 128, 128), 128)
    zlane = pl.ds(pl.multiple_of(z * 128, 128), 128)
    zwide = pl.ds(pl.multiple_of(z * 512, 512), 512)

    def first_hop(p):
        qa, qb = 2 * p, 2 * p + 1
        turn(qa)
        turn(qb)
        for j in (1, 2, 3):
            to = lax.rem(x + j, 4)
            remote(turned.at[qa, :, to], relay.at[qa, :, :, xlane], one_send, one_recv.at[qa], xdev(j))
            to = lax.rem(z + j, 4)
            remote(turned.at[qb, to], relay.at[qb, :, :, zlane], one_send, one_recv.at[qb], zdev(j))
        relay[qa, :, :, xlane] = turned[qa, :, x]
        relay[qb, :, :, zlane] = turned[qb, z]

    def second_hop(p):
        qa, qb = 2 * p, 2 * p + 1
        ea = (qa // HALF) * 16 + c * HALF + lax.rem(qa, HALF)
        eb = ea + 1
        wait_bytes(relay.at[qa, pl.ds(0, 3)], one_recv.at[qa])
        wait_bytes(relay.at[qb, pl.ds(0, 3)], one_recv.at[qb])
        for j in (1, 2, 3, 0):
            tz, tx = lax.rem(z + j, 4), lax.rem(x + j, 4)
            for cc in (c, oc):
                rows = pl.ds(pl.multiple_of(cc * 32, 32), 32)
                if j == 0 and cc is c:
                    out[ea, :, zwide] = relay[qa, z, rows]
                    for s in range(4):
                        at = pl.ds(pl.multiple_of(s * 512 + x * 128, 128), 128)
                        out[eb, :, at] = relay[qb, x, rows, s * 128 : (s + 1) * 128]
                    continue
                other_core = {} if cc is c else {"c": oc}
                remote(
                    relay.at[qa, tz, rows], out.at[ea, :, zwide], two_send, two_recv,
                    {**zdev(j), **other_core} if j else other_core,
                )
                for s in range(4):
                    at = pl.ds(pl.multiple_of(s * 512 + x * 128, 128), 128)
                    remote(
                        relay.at[qb, tx, rows, pl.ds(s * 128, 128)], out.at[eb, :, at], two_send, two_recv,
                        {**xdev(j), **other_core} if j else other_core,
                    )

    place = b * 2 + c
    chip = pl.ds(pl.multiple_of((z * 4 + x) * 128, 128), 128)

    def router_start():
        wait_bytes(swap.at[1, 0], rt_recv.at[0])
        lane = lax.broadcasted_iota(jnp.int32, (HALF, 128), 1)
        own = (lane < 64) == (c == 0)
        part[...] = jnp.where(own, swap[0, c], swap[1, 0]).astype(BF16)
        router[place, :, chip] = part[...]
        for j in (1, 2, 3):
            remote(part, router.at[place, :, chip], rt_send.at[1], rt_recv.at[1], xdev(j))

    def router_z():
        wait_bytes(router.at[place, :, pl.ds(0, 384)], rt_recv.at[1])
        for j in (1, 2, 3):
            remote(
                router.at[place, :, zwide], router.at[place, :, zwide], rt_send.at[2], rt_recv.at[2], zdev(j)
            )

    def router_y():
        wait_bytes(router.at[place, :, pl.ds(0, 1536)], rt_recv.at[2])
        for j in (1, 2, 3):
            remote(
                router.at[place], router.at[place], rt_send.at[3], rt_recv.at[3], {"b": lax.rem(b + j, 4)}
            )

    def router_core():
        wait_bytes(router.at[pl.ds(0, 3)], rt_recv.at[3])
        for j in range(4):
            remote(router.at[2 * j + c], router.at[2 * j + c], rt_send.at[4], rt_recv.at[4], {"c": oc})

    sums(0)
    sums(1)
    fold_x(0)
    sums(2)
    fold_z(0)
    first_hop(0)
    fold_x(1)
    sums(3)
    fold_z(1)
    first_hop(1)
    fold_x(2)
    fold_x(3)
    router_start()
    first_hop(2)
    second_hop(0)
    fold_z(2)
    fold_z(3)
    remote(scale, other, sc_send, sc_recv, {"c": oc})
    router_z()

    def step(p, carry):
        first_hop(p)
        second_hop(p - LAG)
        return carry

    lax.fori_loop(3, 6, step, 0)
    router_y()
    lax.fori_loop(6, 9, step, 0)
    router_core()
    lax.fori_loop(9, PAIRS, step, 0)

    wait_bytes(scale, sc_recv)
    wait_bytes(scale, sc_send)
    index = (z * 4 + x) * 2 + c
    turn_by = lax.rem(4 - lax.rem(index, 4), 4) * 32
    column = pl.ds(pl.multiple_of((index // 4) * 128, 128), 128)

    def emit(q, carry):
        row = (q // HALF) * 16 + lax.rem(q, HALF)
        scales[row + c * HALF] = pltpu.roll(scale[q, :, column], turn_by, 1)
        scales[row + oc * HALF] = pltpu.roll(other[q, :, column], turn_by, 1)
        return carry

    lax.fori_loop(0, SLOTS, emit, 0)

    for p in range(PAIRS - LAG, PAIRS):
        second_hop(p)

    wait_bytes(router.at[pl.ds(0, 4)], rt_recv.at[4])
    wait_bytes(swap.at[1, 0], rt_send.at[0])
    wait_bytes(router.at[place, :, pl.ds(0, 384)], rt_send.at[1])
    wait_bytes(router.at[place, :, pl.ds(0, 1536)], rt_send.at[2])
    wait_bytes(router.at[pl.ds(0, 3)], rt_send.at[3])
    wait_bytes(router.at[pl.ds(0, 4)], rt_send.at[4])
    for k, (first, n) in enumerate(GROUPS):
        wait_bytes(full.at[pl.ds(first, n), mine], core_send.at[k])
        wait_bytes(xsum.at[pl.ds(0, 3), pl.ds(first, n)], xs_send.at[k])
        wait_bytes(zsum.at[pl.ds(0, 3), pl.ds(first, n)], zs_send.at[k])
    wait_bytes(turned.at[pl.ds(0, SLOTS * 3 // 4)], one_send)
    wait_bytes(out.at[pl.ds(0, 42)], two_send)
    wait_bytes(out.at[pl.ds(0, 42)], two_recv)


def body(train_gate, train_up, train_down, router_weight, router_gain):
    vmem = pl.BlockSpec(memory_space=pltpu.VMEM)
    anywhere = pl.BlockSpec(memory_space=pl.ANY)
    dma = pltpu.SemaphoreType.DMA
    groups = len(GROUPS)
    out, scales, router = pl.pallas_call(
        kernel,
        out_shape=(
            jax.ShapeDtypeStruct((48, 32, 2048), BF16),
            jax.ShapeDtypeStruct((48, 1, 128), F32),
            jax.ShapeDtypeStruct((8, 8, 2048), BF16),
        ),
        in_specs=[anywhere] * 3 + [vmem] * 2,
        out_specs=(vmem, vmem, vmem),
        scratch_shapes=[
            pltpu.VMEM((SLOTS, 128, 1024), F32),
            pltpu.VMEM((SLOTS, 4, 4, 64, 128), BF16),
            pltpu.VMEM((SLOTS, 4, 64, 512), BF16),
            pltpu.VMEM((4, SLOTS, 1, 1024), F32),
            pltpu.VMEM((4, SLOTS, 1, 1024), F32),
            pltpu.VMEM((SLOTS, 1, 1024), F32),
            pltpu.VMEM((SLOTS, 1, 1024), F32),
            pltpu.VMEM((SLOTS, 1, 1024), F32),
            pltpu.VMEM((2, 2, HALF, 128), F32),
            pltpu.VMEM((HALF, 128), BF16),
            dma((groups,)), dma((groups,)), dma((groups,)), dma((groups,)), dma((groups,)),
            dma((groups,)), dma((groups,)),
            dma, dma((SLOTS,)), dma, dma, dma, dma, dma((5,)), dma((5,)),
        ],
        compiler_params=pltpu.CompilerParams(
            collective_id=0, has_side_effects=True, vmem_limit_bytes=52 * 1024 * 1024
        ),
    )(
        train_gate,
        train_up,
        jnp.transpose(train_down, (0, 2, 1)),
        router_weight.T,
        router_gain.reshape(1, 64),
    )
    ready_gate, ready_up, ready_down = out[:16], out[16:32], out[32:]
    scale_gate, scale_up, scale_down = (scales[16 * t : 16 * t + 16, 0, :32] for t in range(3))
    return (
        jnp.transpose(ready_gate, (0, 2, 1)),
        jnp.transpose(ready_up, (0, 2, 1)),
        ready_down,
        scale_gate,
        scale_up,
        scale_down,
        router.reshape(64, 2048).T,
    )


def solution(mesh):
    split = Mesh(mesh.devices.reshape(mesh.shape["bank"], 4, 4, 2), ("b",) + ZERO)
    return jax.shard_map(
        body,
        mesh=split,
        in_specs=(P("b", ZERO, None), P("b", ZERO, None), P("b", None, ZERO), P(ZERO, "b"), P(ZERO)),
        out_specs=(
            P("b", None, ZERO),
            P("b", None, ZERO),
            P("b", ZERO, None),
            P("b", ZERO),
            P("b", ZERO),
            P("b", ZERO),
            P(),
        ),
        check_vma=False,
    )
```

time: 341 us -> 104 us (0.30)
  waiting for transfers between devices: 110 us -> 0 us
  local copies, waits for them, and re-layouts: 114 us -> 8.46 us
  Pallas kernels: 0 us -> 94.4 us
  blocking collectives: 57 us -> 0 us
  other arithmetic: 25.5 us -> 0 us
  starting transfers between devices: 17.3 us -> 0 us
  between operations: 14.2 us -> 0.65 us
    psum x1 -> x0, waiting for transfers between devices: 98.1 us -> none  [packed_total(): total = lax.psum(jnp.concatenate([a.ravel() for a in arrays]), axis)]
    pallas_call x0 -> x1, Pallas kernels: none -> 94.4 us  [body(): pl.pallas_call(kernel, out_shape=(jax.ShapeDtypeStruct((48, 32, 2048), BF...]
    unnamed x21 -> x5, local copies, waits for them, and re-layouts: 69.7 us -> 2.05 us
    all_gather x3 -> x0, blocking collectives: 57 us -> none  [the longest x2 46.8 us: all_blocks(): pieces = lax.all_gather(pieces, axes[k], axis=0, tiled=True)]
    all_to_all x6 -> x0, local copies, waits for them, and re-layouts: 40.8 us -> none  [the longest x2 13.6 us: body(): lax.all_to_all(narrow_down, ZERO, split_axis=1, concat_axis=2, tiled=True)]
    unnamed x4 -> x0, other arithmetic: 20.6 us -> none
    all_to_all x3 -> x0, starting transfers between devices: 17.2 us -> none  [the longest x1 6.46 us: body(): lax.all_to_all(narrow_down, ZERO, split_axis=1, concat_axis=2, tiled=True)]
    all_to_all x3 -> x0, waiting for transfers between devices: 11.8 us -> none  [the longest x1 6.05 us: body(): lax.all_to_all(narrow_gate, ZERO, split_axis=2, concat_axis=1, tiled=True)]
  transfers between devices with their start and end apart: 4 -> 0, of which waited for: 3 -> 0; matrix products, arithmetic and copies ran while one was open for 24% -> 0% of each run, Pallas kernels for 0% -> 0%
where the time goes in v1:
time: 104 us
  Pallas kernels  94.4 us (91%)
  local copies, waits for them, and re-layouts  8.46 us (8%)
    pallas_call x1, Pallas kernels, body(): pl.pallas_call(kernel, out_shape=(jax.ShapeDtypeStruct((48, 32, 2048), BF...  94.4 us
    slice x1, local copies, waits for them, and re-layouts, body(): ready_gate, ready_up, ready_down = (out[:16], out[16:32], out[32:])  5.81 us

profile of v1, /device:TPU:1, one launch (start us, length us, event | category | flops | bytes accessed | tf_op | source)
XLA Modules:
  0.0 103.6 jit_solution(9732778731243648894)
XLA Ops:
  0.6 0.0 copy-start
  0.6 0.7 copy-done
  1.3 0.0 copy-start.1
  1.3 0.7 copy-done.1
  2.0 94.4 %shard_map.108 = (bf16[48,32,2048]{2,1,0:T(8,128)(2,1)}, f32[48,1,128]{2,1,0:T(1,128)S(1)}, bf16[8,8,2048]{2,1,0:T(8,128)(2,1)S(1)}) custom-call(f32[16,64,1024]{2,1,0:T(8,128)} %gate.1, f32[16,64,1024]{2,1,0:T(8,128)} %up.1, f32[16,64,1024]{2,1,0:T(8,128)} %bitcast.16, f32[16,64]{1,0:T(8,128)S(1)} %bitcast.14, f32[1,64]{1,0:T(1,128)S(1)} %bitcast.15), custom_call_target="tpu_custom_call" | custom-call | tf_op jit(solution)/shard_map/pallas_call | solution.py:255
  96.4 5.8 %fusion = (bf16[16,32,2048]{2,1,0:T(8,128)(2,1)}, bf16[16,2048,32]{1,2,0:T(8,128)(2,1)}, bf16[16,2048,32]{1,2,0:T(8,128)(2,1)}) fusion(bf16[48,32,2048]{2,1,0:T(8,128)(2,1)} %get-tuple-element.10), kind=kLoop, calls=%fused_computation.2 | loop fusion | bytes 12582912 | tf_op jit(solution)/shard_map/slice | solution.py:289
  102.2 0.6 fusion.1
  102.8 0.7 copy.13
Async XLA Ops:
  0.6 0.7 copy-start
  1.3 0.7 copy-start.1

commit v2 on v1

--- a/solution.py
+++ b/solution.py
@@ -16,13 +16,16 @@
 SLOTS = 3 * HALF
 PAIRS = SLOTS // 2
 LAG = 2
-GROUPS = ((0, 2), (2, 6), (8, 8), (16, 8))
+CHUNKS = ((0, 2), (2, 6), (8, 8), (16, 8))
+ALONG_X = (2, 10)
+ALONG_Z = (12, 12)
 
 
 def kernel(
     gate, up, down, weight, gain, out, scales, router,
-    full, turned, relay, xsum, zsum, scale, other, inverse, swap, part,
-    load_sem, core_send, core_recv, xs_send, xs_recv, zs_send, zs_recv,
+    full, half, turned, relay, own_sum, lent_sum, got_sum, pair_sum, stage_one, stage_two,
+    scale, other, inverse, swap, part, weight_in, gain_in,
+    load_sem, core_send, core_recv, sum_send, sum_recv,
     one_send, one_recv, two_send, two_recv, sc_send, sc_recv, rt_send, rt_recv,
 ):
     b, z, x, c = (lax.axis_index(n) for n in ("b", "z", "x", "c"))
@@ -41,15 +44,6 @@
 
     def wait_bytes(ref, sem):
         pltpu.make_async_copy(ref, ref, sem).wait()
-
-    sources = (gate, up, down)
-    mine = pl.ds(pl.multiple_of(c * 64, 64), 64)
-
-    for k, (first, n) in enumerate(GROUPS):
-        src = sources[first // HALF]
-        pltpu.make_async_copy(
-            src.at[pl.ds(c * HALF + first % HALF, n)], full.at[pl.ds(first, n), mine], load_sem.at[k]
-        ).start()
 
     barrier = pltpu.get_barrier_semaphore()
     peers = [{"c": oc}]
@@ -58,48 +52,88 @@
     for dev in peers:
         pl.semaphore_signal(barrier, inc=1, device_id=dev, device_id_type=MESH)
 
-    product = weight[...] * gain[...]
+    sources = (gate, up, down)
+    mine = pl.ds(pl.multiple_of(c * 64, 64), 64)
+
+    loads = []
+    for k, (first, n) in enumerate(CHUNKS):
+        src, at = sources[first // HALF], pl.ds(first, n)
+        loads.append((
+            pltpu.make_async_copy(
+                src.at[pl.ds(c * HALF + first % HALF, n)], full.at[at, mine], load_sem.at[2 * k]
+            ),
+            pltpu.make_async_copy(
+                src.at[pl.ds(oc * HALF + first % HALF, n)], half.at[at], load_sem.at[2 * k + 1]
+            ),
+        ))
+    loads.append((
+        pltpu.make_async_copy(weight, weight_in, load_sem.at[2 * len(CHUNKS)]),
+        pltpu.make_async_copy(gain, gain_in, load_sem.at[2 * len(CHUNKS) + 1]),
+    ))
+    for pair in loads:
+        for copy in pair:
+            copy.start()
+
+    def own_sums(k):
+        first, n = CHUNKS[k]
+        for copy in loads[k]:
+            copy.wait()
+
+        def one(q, carry):
+            rows = full[q, mine]
+            own_sum[q] = jnp.sum(rows * rows, axis=0, keepdims=True)
+            rows = half[q]
+            lent_sum[q] = jnp.sum(rows * rows, axis=0, keepdims=True)
+            return carry
+
+        lax.fori_loop(first, first + n, one, 0)
+
+    own_sums(0)
+    lead = pl.ds(0, 2)
+    pair_sum[x * 2 + c] = own_sum[lead]
+    pl.semaphore_wait(barrier, len(peers))
+
+    here = x * 2 + c
+    for j in (1, 2, 3):
+        remote(pair_sum.at[here], pair_sum.at[here], sum_send.at[0], sum_recv.at[0], xdev(j))
+    for j in (1, 2, 3):
+        remote(lent_sum.at[lead], pair_sum.at[here], sum_send.at[0], sum_recv.at[0], {**xdev(j), "c": oc})
+    remote(lent_sum.at[lead], pair_sum.at[here], sum_send.at[0], sum_recv.at[0], {"c": oc})
+    for k in range(1, len(CHUNKS)):
+        own_sums(k)
+
+    def lend(k):
+        first, n = CHUNKS[k]
+        at = pl.ds(first, n)
+        remote(half.at[at], full.at[at, mine], core_send.at[k], core_recv.at[k], {"c": oc})
+
+    rest = pl.ds(2, SLOTS - 2)
+    remote(lent_sum.at[rest], got_sum.at[rest], sum_send.at[1], sum_recv.at[1], {"c": oc})
+    for k in range(len(CHUNKS)):
+        lend(k)
+
+    for copy in loads[-1]:
+        copy.wait()
+    product = weight_in[...] * gain_in[...]
     swap[0] = jnp.concatenate([product, product], axis=1).reshape(2, HALF, 128)
-    pl.semaphore_wait(barrier, len(peers))
-
-    for k, (first, n) in enumerate(GROUPS):
-        src = sources[first // HALF]
-        remote(
-            src.at[pl.ds(oc * HALF + first % HALF, n)], full.at[pl.ds(first, n), mine],
-            core_send.at[k], core_recv.at[k], {"c": oc},
-        )
+
+    wait_bytes(pair_sum.at[pl.ds(0, 7)], sum_recv.at[0])
+    total = [pair_sum[2 * k] + pair_sum[2 * k + 1] for k in range(4)]
+    stage_two[z, lead] = (total[0] + total[1]) + (total[2] + total[3])
+    for j in (1, 2, 3):
+        remote(stage_two.at[z, lead], stage_two.at[z, lead], sum_send.at[2], sum_recv.at[2], zdev(j))
+
+    wait_bytes(lent_sum.at[rest], sum_recv.at[1])
+    plans = ((ALONG_X, x, xdev, z, zdev, 3, 5), (ALONG_Z, z, zdev, x, xdev, 4, 6))
+    for (first, n), me, dev, _, _, sem, _ in plans:
+        at = pl.ds(first, n)
+        stage_one[me, at] = own_sum[at] + got_sum[at]
+        for j in (1, 2, 3):
+            remote(stage_one.at[me, at], stage_one.at[me, at], sum_send.at[sem], sum_recv.at[sem], dev(j))
     remote(swap.at[0, oc], swap.at[1, 0], rt_send.at[0], rt_recv.at[0], {"c": oc})
 
-    def sums(k):
-        first, n = GROUPS[k]
-        pltpu.make_async_copy(
-            gate.at[pl.ds(0, n)], full.at[pl.ds(first, n), mine], load_sem.at[k]
-        ).wait()
-        wait_bytes(full.at[pl.ds(first, n), mine], core_recv.at[k])
-
-        def one(q, carry):
-            rows = full[q]
-            xsum[x, q] = jnp.sum(rows * rows, axis=0, keepdims=True)
-            return carry
-
-        lax.fori_loop(first, first + n, one, 0)
-        at = pl.ds(first, n)
-        for j in (1, 2, 3):
-            remote(xsum.at[x, at], xsum.at[x, at], xs_send.at[k], xs_recv.at[k], xdev(j))
-
-    def fold_x(k):
-        first, n = GROUPS[k]
-        at = pl.ds(first, n)
-        wait_bytes(xsum.at[pl.ds(0, 3), at], xs_recv.at[k])
-        zsum[z, at] = (xsum[0, at] + xsum[1, at]) + (xsum[2, at] + xsum[3, at])
-        for j in (1, 2, 3):
-            remote(zsum.at[z, at], zsum.at[z, at], zs_send.at[k], zs_recv.at[k], zdev(j))
-
-    def fold_z(k):
-        first, n = GROUPS[k]
-        at = pl.ds(first, n)
-        wait_bytes(zsum.at[pl.ds(0, 3), at], zs_recv.at[k])
-        root = jnp.sqrt((zsum[0, at] + zsum[1, at]) + (zsum[2, at] + zsum[3, at]))
+    def finish(at):
+        root = jnp.sqrt((stage_two[0, at] + stage_two[1, at]) + (stage_two[2, at] + stage_two[3, at]))
         scale[at] = root
         inverse[at] = 1.0 / root
 
@@ -116,10 +150,11 @@
     def first_hop(p):
         qa, qb = 2 * p, 2 * p + 1
         turn(qa)
-        turn(qb)
         for j in (1, 2, 3):
             to = lax.rem(x + j, 4)
             remote(turned.at[qa, :, to], relay.at[qa, :, :, xlane], one_send, one_recv.at[qa], xdev(j))
+        turn(qb)
+        for j in (1, 2, 3):
             to = lax.rem(z + j, 4)
             remote(turned.at[qb, to], relay.at[qb, :, :, zlane], one_send, one_recv.at[qb], zdev(j))
         relay[qa, :, :, xlane] = turned[qa, :, x]
@@ -184,36 +219,42 @@
         for j in range(4):
             remote(router.at[2 * j + c], router.at[2 * j + c], rt_send.at[4], rt_recv.at[4], {"c": oc})
 
-    sums(0)
-    sums(1)
-    fold_x(0)
-    sums(2)
-    fold_z(0)
+    wait_bytes(full.at[lead, mine], core_recv.at[0])
+    wait_bytes(stage_two.at[pl.ds(0, 3), lead], sum_recv.at[2])
+    finish(lead)
     first_hop(0)
-    fold_x(1)
-    sums(3)
-    fold_z(1)
+    for (first, n), _, _, me, dev, before, sem in plans:
+        at = pl.ds(first, n)
+        wait_bytes(stage_one.at[pl.ds(0, 3), at], sum_recv.at[before])
+        stage_two[me, at] = (stage_one[0, at] + stage_one[1, at]) + (stage_one[2, at] + stage_one[3, at])
+        for j in (1, 2, 3):
+            remote(stage_two.at[me, at], stage_two.at[me, at], sum_send.at[sem], sum_recv.at[sem], dev(j))
+    router_start()
+    for (first, n), _, _, _, _, _, sem in plans:
+        at = pl.ds(first, n)
+        wait_bytes(stage_two.at[pl.ds(0, 3), at], sum_recv.at[sem])
+        finish(at)
+    wait_bytes(full.at[pl.ds(2, 6), mine], core_recv.at[1])
     first_hop(1)
-    fold_x(2)
-    fold_x(3)
-    router_start()
+    remote(scale, other, sc_send, sc_recv, {"c": oc})
+    router_z()
     first_hop(2)
     second_hop(0)
-    fold_z(2)
-    fold_z(3)
-    remote(scale, other, sc_send, sc_recv, {"c": oc})
-    router_z()
 
     def step(p, carry):
         first_hop(p)
         second_hop(p - LAG)
         return carry
 
-    lax.fori_loop(3, 6, step, 0)
+    step(3, 0)
+    wait_bytes(full.at[pl.ds(8, 8), mine], core_recv.at[2])
+    lax.fori_loop(4, 6, step, 0)
     router_y()
-    lax.fori_loop(6, 9, step, 0)
+    lax.fori_loop(6, 8, step, 0)
+    wait_bytes(full.at[pl.ds(16, 8), mine], core_recv.at[3])
+    lax.fori_loop(8, 10, step, 0)
     router_core()
-    lax.fori_loop(9, PAIRS, step, 0)
+    lax.fori_loop(10, PAIRS, step, 0)
 
     wait_bytes(scale, sc_recv)
     wait_bytes(scale, sc_send)
@@ -223,8 +264,8 @@
 
     def emit(q, carry):
         row = (q // HALF) * 16 + lax.rem(q, HALF)
-        scales[row + c * HALF] = pltpu.roll(scale[q, :, column], turn_by, 1)
-        scales[row + oc * HALF] = pltpu.roll(other[q, :, column], turn_by, 1)
+        scales[row + c * HALF] = pltpu.roll(scale[q, :, column], turn_by, 1)[:, :32]
+        scales[row + oc * HALF] = pltpu.roll(other[q, :, column], turn_by, 1)[:, :32]
         return carry
 
     lax.fori_loop(0, SLOTS, emit, 0)
@@ -238,64 +279,104 @@
     wait_bytes(router.at[place, :, pl.ds(0, 1536)], rt_send.at[2])
     wait_bytes(router.at[pl.ds(0, 3)], rt_send.at[3])
     wait_bytes(router.at[pl.ds(0, 4)], rt_send.at[4])
-    for k, (first, n) in enumerate(GROUPS):
+    for k, (first, n) in enumerate(CHUNKS):
         wait_bytes(full.at[pl.ds(first, n), mine], core_send.at[k])
-        wait_bytes(xsum.at[pl.ds(0, 3), pl.ds(first, n)], xs_send.at[k])
-        wait_bytes(zsum.at[pl.ds(0, 3), pl.ds(first, n)], zs_send.at[k])
+    wait_bytes(pair_sum.at[pl.ds(0, 7)], sum_send.at[0])
+    wait_bytes(lent_sum.at[rest], sum_send.at[1])
+    wait_bytes(stage_two.at[pl.ds(0, 3), lead], sum_send.at[2])
+    for (first, n), _, _, _, _, before, sem in plans:
+        wait_bytes(stage_one.at[pl.ds(0, 3), pl.ds(first, n)], sum_send.at[before])
+        wait_bytes(stage_two.at[pl.ds(0, 3), pl.ds(first, n)], sum_send.at[sem])
     wait_bytes(turned.at[pl.ds(0, SLOTS * 3 // 4)], one_send)
     wait_bytes(out.at[pl.ds(0, 42)], two_send)
     wait_bytes(out.at[pl.ds(0, 42)], two_recv)
 
 
+def writer(packed, scales, router, *rest):
+    results, sem = rest[:-1], rest[-1]
+    copies = []
+    for t in range(3):
+        for k in range(0, 16, 4):
+            copies.append((packed.at[pl.ds(16 * t + k, 4)], results[t].at[pl.ds(k, 4)]))
+    for t in range(3):
+        copies.append((scales.at[pl.ds(16 * t, 16)], results[3 + t]))
+    copies.append((router, results[6]))
+    copies = [pltpu.make_async_copy(src, dst, sem.at[k]) for k, (src, dst) in enumerate(copies)]
+    for copy in copies:
+        copy.start()
+    for copy in copies:
+        copy.wait()
+
+
 def body(train_gate, train_up, train_down, router_weight, router_gain):
     vmem = pl.BlockSpec(memory_space=pltpu.VMEM)
-    anywhere = pl.BlockSpec(memory_space=pl.ANY)
+    hbm = pl.BlockSpec(memory_space=pltpu.HBM)
     dma = pltpu.SemaphoreType.DMA
-    groups = len(GROUPS)
-    out, scales, router = pl.pallas_call(
+    chunks = len(CHUNKS)
+    sums = (SLOTS, 1, 1024)
+    packed, scales, router = pl.pallas_call(
         kernel,
         out_shape=(
-            jax.ShapeDtypeStruct((48, 32, 2048), BF16),
-            jax.ShapeDtypeStruct((48, 1, 128), F32),
-            jax.ShapeDtypeStruct((8, 8, 2048), BF16),
+            pltpu.VMEM((48, 32, 2048), BF16),
+            pltpu.VMEM((48, 1, 32), F32),
+            pltpu.VMEM((8, 8, 2048), BF16),
         ),
-        in_specs=[anywhere] * 3 + [vmem] * 2,
+        in_specs=[hbm] * 5,
         out_specs=(vmem, vmem, vmem),
         scratch_shapes=[
             pltpu.VMEM((SLOTS, 128, 1024), F32),
+            pltpu.VMEM((SLOTS, 64, 1024), F32),
             pltpu.VMEM((SLOTS, 4, 4, 64, 128), BF16),
             pltpu.VMEM((SLOTS, 4, 64, 512), BF16),
-            pltpu.VMEM((4, SLOTS, 1, 1024), F32),
-            pltpu.VMEM((4, SLOTS, 1, 1024), F32),
-            pltpu.VMEM((SLOTS, 1, 1024), F32),
-            pltpu.VMEM((SLOTS, 1, 1024), F32),
-            pltpu.VMEM((SLOTS, 1, 1024), F32),
+            pltpu.VMEM(sums, F32),
+            pltpu.VMEM(sums, F32),
+            pltpu.VMEM(sums, F32),
+            pltpu.VMEM((8, 2, 1, 1024), F32),
+            pltpu.VMEM((4,) + sums, F32),
+            pltpu.VMEM((4,) + sums, F32),
+            pltpu.VMEM(sums, F32),
+            pltpu.VMEM(sums, F32),
+            pltpu.VMEM(sums, F32),
             pltpu.VMEM((2, 2, HALF, 128), F32),
             pltpu.VMEM((HALF, 128), BF16),
-            dma((groups,)), dma((groups,)), dma((groups,)), dma((groups,)), dma((groups,)),
-            dma((groups,)), dma((groups,)),
+            pltpu.VMEM((16, 64), F32),
+            pltpu.VMEM((1, 64), F32),
+            dma((2 * chunks + 2,)), dma((chunks,)), dma((chunks,)), dma((7,)), dma((7,)),
             dma, dma((SLOTS,)), dma, dma, dma, dma, dma((5,)), dma((5,)),
         ],
         compiler_params=pltpu.CompilerParams(
-            collective_id=0, has_side_effects=True, vmem_limit_bytes=52 * 1024 * 1024
+            collective_id=0, has_side_effects=True, vmem_limit_bytes=56 * 1024 * 1024
         ),
     )(
-        train_gate,
-        train_up,
-        jnp.transpose(train_down, (0, 2, 1)),
-        router_weight.T,
-        router_gain.reshape(1, 64),
+        *(
+            pltpu.with_memory_space_constraint(a, pltpu.HBM)
+            for a in (
+                train_gate,
+                train_up,
+                jnp.transpose(train_down, (0, 2, 1)),
+                router_weight.T,
+                router_gain.reshape(1, 64),
+            )
+        )
     )
-    ready_gate, ready_up, ready_down = out[:16], out[16:32], out[32:]
-    scale_gate, scale_up, scale_down = (scales[16 * t : 16 * t + 16, 0, :32] for t in range(3))
+    tensor = jax.ShapeDtypeStruct((16, 32, 2048), BF16)
+    column = jax.ShapeDtypeStruct((16, 1, 32), F32)
+    ready_gate, ready_up, ready_down, scale_gate, scale_up, scale_down, serve_router = pl.pallas_call(
+        writer,
+        out_shape=(tensor,) * 3 + (column,) * 3 + (jax.ShapeDtypeStruct((8, 8, 2048), BF16),),
+        in_specs=[vmem] * 3,
+        out_specs=(hbm,) * 7,
+        scratch_shapes=[dma((16,))],
+        compiler_params=pltpu.CompilerParams(vmem_limit_bytes=1024 * 1024),
+    )(packed, scales, router)
     return (
         jnp.transpose(ready_gate, (0, 2, 1)),
         jnp.transpose(ready_up, (0, 2, 1)),
         ready_down,
-        scale_gate,
-        scale_up,
-        scale_down,
-        router.reshape(64, 2048).T,
+        scale_gate.reshape(16, 32),
+        scale_up.reshape(16, 32),
+        scale_down.reshape(16, 32),
+        serve_router.reshape(64, 2048).T,
     )
 
 

time: 104 us -> 92.8 us (0.89)
  local copies, waits for them, and re-layouts: 8.46 us -> 0 us
  Pallas kernels: 94.4 us -> 92 us
    slice x2 -> x0, local copies, waits for them, and re-layouts: 6.42 us -> none  [the longest x1 5.81 us: body(): ready_gate, ready_up, ready_down = (out[:16], out[16:32], out[32:])]
    pallas_call x1 -> x2, Pallas kernels: 94.4 us -> 92 us  [the longest x1 89.2 us: body(): pl.pallas_call(kernel, out_shape=(pltpu.VMEM((48, 32, 2048), BF16), pltpu...]
    unnamed x5 -> x0, local copies, waits for them, and re-layouts: 2.05 us -> none
where the time goes in v2:
time: 92.8 us; the launch traced here: 92.7 us
  Pallas kernels  92 us (99%)
    pallas_call x1, Pallas kernels, body(): pl.pallas_call(kernel, out_shape=(pltpu.VMEM((48, 32, 2048), BF16), pltpu...  89.2 us
    pallas_call x1, Pallas kernels, body(): pl.pallas_call(writer, out_shape=(tensor,) * 3 + (column,) * 3 + (jax.Sha...  2.87 us

profile of v2, /device:TPU:1, one launch (start us, length us, event | category | flops | bytes accessed | tf_op | source)
XLA Modules:
  0.0 92.7 jit_solution(3104761321480456015)
XLA Ops:
  0.6 89.2 %shard_map.108 = (bf16[48,32,2048]{2,1,0:T(8,128)(2,1)S(1)}, f32[48,1,32]{2,1,0:T(1,128)S(1)}, bf16[8,8,2048]{2,1,0:T(8,128)(2,1)S(1)}) custom-call(f32[16,64,1024]{2,1,0:T(8,128)} %gate.1, f32[16,64,1024]{2,1,0:T(8,128)} %up.1, f32[16,64,1024]{2,1,0:T(8,128)} %bitcast.11, f32[16,64]{1,0:T(8,128)} %bitcast.12, f32[1,64]{1,0:T(1,128)} %bitcast.13), custom_call_target="tpu_custom_call" | custom-call | tf_op jit(solution)/shard_map/pallas_call | solution.py:317
  89.8 2.9 %shard_map.109 = (bf16[16,32,2048]{2,1,0:T(8,128)(2,1)}, bf16[16,32,2048]{2,1,0:T(8,128)(2,1)}, bf16[16,32,2048]{2,1,0:T(8,128)(2,1)}, f32[16,1,32]{2,1,0:T(1,12...) custom-call(bf16[48,32,2048]{2,1,0:T(8,128)(2,1)S(1)} %get-tuple-element.17.packed, ...), custom_call_target="tpu_custom_call" | custom-call | tf_op jit(solution)/shard_map/pallas_call | solution.py:364

commit v3 on v2

--- a/solution.py
+++ b/solution.py
@@ -17,15 +17,15 @@
 PAIRS = SLOTS // 2
 LAG = 2
 CHUNKS = ((0, 2), (2, 6), (8, 8), (16, 8))
-ALONG_X = (2, 10)
-ALONG_Z = (12, 12)
+LEAD = 8
+LATER = ((8, 8), (16, 8))
 
 
 def kernel(
     gate, up, down, weight, gain, out, scales, router,
-    full, half, turned, relay, own_sum, lent_sum, got_sum, pair_sum, stage_one, stage_two,
-    scale, other, inverse, swap, part, weight_in, gain_in,
-    load_sem, core_send, core_recv, sum_send, sum_recv,
+    full, half, turned, relay, raw, raw_relay, spread, own_sum, lent_sum, got_sum, chip_sum,
+    lead_x, lead_z, quarter_one, quarter_two, total, scale, other, inverse, swap, part, weight_in, gain_in,
+    load_sem, core_send, core_recv, sum_send, sum_recv, raw_send, raw_recv,
     one_send, one_recv, two_send, two_recv, sc_send, sc_recv, rt_send, rt_recv,
 ):
     b, z, x, c = (lax.axis_index(n) for n in ("b", "z", "x", "c"))
@@ -74,11 +74,12 @@
         for copy in pair:
             copy.start()
 
+    def arrived(k):
+        for copy in loads[k]:
+            copy.wait()
+
     def own_sums(k):
         first, n = CHUNKS[k]
-        for copy in loads[k]:
-            copy.wait()
-
         def one(q, carry):
             rows = full[q, mine]
             own_sum[q] = jnp.sum(rows * rows, axis=0, keepdims=True)
@@ -88,54 +89,84 @@
 
         lax.fori_loop(first, first + n, one, 0)
 
+    arrived(0)
     own_sums(0)
-    lead = pl.ds(0, 2)
-    pair_sum[x * 2 + c] = own_sum[lead]
+    arrived(1)
+    own_sums(1)
+    arrived(2)
+    arrived(3)
     pl.semaphore_wait(barrier, len(peers))
 
-    here = x * 2 + c
-    for j in (1, 2, 3):
-        remote(pair_sum.at[here], pair_sum.at[here], sum_send.at[0], sum_recv.at[0], xdev(j))
-    for j in (1, 2, 3):
-        remote(lent_sum.at[lead], pair_sum.at[here], sum_send.at[0], sum_recv.at[0], {**xdev(j), "c": oc})
-    remote(lent_sum.at[lead], pair_sum.at[here], sum_send.at[0], sum_recv.at[0], {"c": oc})
-    for k in range(1, len(CHUNKS)):
-        own_sums(k)
-
-    def lend(k):
-        first, n = CHUNKS[k]
+    lead, later = pl.ds(0, LEAD), pl.ds(LEAD, SLOTS - LEAD)
+    remote(lent_sum.at[lead], got_sum.at[lead], sum_send.at[0], sum_recv.at[0], {"c": oc})
+    for k, (first, n) in enumerate(CHUNKS):
         at = pl.ds(first, n)
         remote(half.at[at], full.at[at, mine], core_send.at[k], core_recv.at[k], {"c": oc})
-
-    rest = pl.ds(2, SLOTS - 2)
-    remote(lent_sum.at[rest], got_sum.at[rest], sum_send.at[1], sum_recv.at[1], {"c": oc})
-    for k in range(len(CHUNKS)):
-        lend(k)
-
     for copy in loads[-1]:
         copy.wait()
     product = weight_in[...] * gain_in[...]
     swap[0] = jnp.concatenate([product, product], axis=1).reshape(2, HALF, 128)
 
-    wait_bytes(pair_sum.at[pl.ds(0, 7)], sum_recv.at[0])
-    total = [pair_sum[2 * k] + pair_sum[2 * k + 1] for k in range(4)]
-    stage_two[z, lead] = (total[0] + total[1]) + (total[2] + total[3])
-    for j in (1, 2, 3):
-        remote(stage_two.at[z, lead], stage_two.at[z, lead], sum_send.at[2], sum_recv.at[2], zdev(j))
-
-    wait_bytes(lent_sum.at[rest], sum_recv.at[1])
-    plans = ((ALONG_X, x, xdev, z, zdev, 3, 5), (ALONG_Z, z, zdev, x, xdev, 4, 6))
-    for (first, n), me, dev, _, _, sem, _ in plans:
-        at = pl.ds(first, n)
-        stage_one[me, at] = own_sum[at] + got_sum[at]
-        for j in (1, 2, 3):
-            remote(stage_one.at[me, at], stage_one.at[me, at], sum_send.at[sem], sum_recv.at[sem], dev(j))
-    remote(swap.at[0, oc], swap.at[1, 0], rt_send.at[0], rt_recv.at[0], {"c": oc})
+    xlane = pl.ds(pl.multiple_of(x * 128, 128), 128)
+    zlane = pl.ds(pl.multiple_of(z * 128, 128), 128)
+
+    def four(ref, *at):
+        return (ref[0, *at] + ref[1, *at]) + (ref[2, *at] + ref[3, *at])
+
+    def to_peers(ref, at, sem, dev):
+        for j in (1, 2, 3):
+            remote(ref.at[at], ref.at[at], sum_send.at[sem], sum_recv.at[sem], dev(j))
+
+    def scatter():
+        for g, ((first, n), me, dev) in enumerate(zip(LATER, (x, z), (xdev, zdev))):
+            quarter_one[g, me] = chip_sum[pl.ds(first + 2 * me, 2)]
+            for j in (1, 2, 3):
+                to = lax.rem(me + j, 4)
+                remote(
+                    chip_sum.at[pl.ds(first + 2 * to, 2)], quarter_one.at[g, me],
+                    sum_send.at[4 + g], sum_recv.at[4 + g], dev(j),
+                )
+
+    def across():
+        for g, (me, dev) in enumerate(zip((z, x), (zdev, xdev))):
+            wait_bytes(quarter_one.at[g, pl.ds(0, 3)], sum_recv.at[4 + g])
+            quarter_two[g, me] = four(quarter_one.at[g])
+            for j in (1, 2, 3):
+                remote(
+                    quarter_two.at[g, me], quarter_two.at[g, me], sum_send.at[6 + g], sum_recv.at[6 + g], dev(j)
+                )
+
+    def back():
+        for g, ((first, n), me, dev) in enumerate(zip(LATER, (x, z), (xdev, zdev))):
+            wait_bytes(quarter_two.at[g, pl.ds(0, 3)], sum_recv.at[6 + g])
+            at = pl.ds(first + 2 * me, 2)
+            total[at] = four(quarter_two.at[g])
+            to_peers(total, at, 8 + g, dev)
 
     def finish(at):
-        root = jnp.sqrt((stage_two[0, at] + stage_two[1, at]) + (stage_two[2, at] + stage_two[3, at]))
+        root = jnp.sqrt(total[at])
         scale[at] = root
         inverse[at] = 1.0 / root
+
+    def turn_raw(q):
+        for j in range(8):
+            block = full[q, :, j * 128 : (j + 1) * 128]
+            raw[q, j // 2, (j % 2) * 2 : (j % 2) * 2 + 2] = block.T.reshape(2, 64, 128)
+
+    def send_raw_z(j):
+        remote(raw.at[1, lax.rem(z + j, 4)], raw_relay.at[1, :, :, zlane], raw_send, raw_recv.at[1], zdev(j))
+
+    def normalise_raw():
+        for q, place in ((0, lambda k: k * 4 + x), (1, lambda k: z * 4 + k)):
+            for j in range(8):
+                row = inverse[q, :, j * 128 : (j + 1) * 128]
+                spread[2 * j : 2 * j + 2] = jnp.broadcast_to(row, (128, 128)).T.reshape(2, 64, 128)
+            wait_bytes(raw_relay.at[q, pl.ds(0, 3)], raw_recv.at[q])
+            for k in range(4):
+                factor = spread[place(k)]
+                for s in range(4):
+                    lanes = slice(s * 128, (s + 1) * 128)
+                    relay[q, k, :, lanes] = (raw_relay[q, k, :, lanes] * factor).astype(BF16)
 
     def turn(q):
         for j in range(8):
@@ -143,8 +174,6 @@
             block = (full[q, :, lanes] * inverse[q, :, lanes]).astype(BF16)
             turned[q, j // 2, (j % 2) * 2 : (j % 2) * 2 + 2] = block.T.reshape(2, 64, 128)
 
-    xlane = pl.ds(pl.multiple_of(x * 128, 128), 128)
-    zlane = pl.ds(pl.multiple_of(z * 128, 128), 128)
     zwide = pl.ds(pl.multiple_of(z * 512, 512), 512)
 
     def first_hop(p):
@@ -164,8 +193,11 @@
         qa, qb = 2 * p, 2 * p + 1
         ea = (qa // HALF) * 16 + c * HALF + lax.rem(qa, HALF)
         eb = ea + 1
-        wait_bytes(relay.at[qa, pl.ds(0, 3)], one_recv.at[qa])
-        wait_bytes(relay.at[qb, pl.ds(0, 3)], one_recv.at[qb])
+        if isinstance(p, int) and p == 0:
+            normalise_raw()
+        else:
+            wait_bytes(relay.at[qa, pl.ds(0, 3)], one_recv.at[qa])
+            wait_bytes(relay.at[qb, pl.ds(0, 3)], one_recv.at[qb])
         for j in (1, 2, 3, 0):
             tz, tx = lax.rem(z + j, 4), lax.rem(x + j, 4)
             for cc in (c, oc):
@@ -219,34 +251,56 @@
         for j in range(4):
             remote(router.at[2 * j + c], router.at[2 * j + c], rt_send.at[4], rt_recv.at[4], {"c": oc})
 
-    wait_bytes(full.at[lead, mine], core_recv.at[0])
-    wait_bytes(stage_two.at[pl.ds(0, 3), lead], sum_recv.at[2])
+    wait_bytes(lent_sum.at[lead], sum_recv.at[0])
+    lead_x[x] = own_sum[lead] + got_sum[lead]
+    to_peers(lead_x, x, 2, xdev)
+
+    wait_bytes(full.at[pl.ds(0, 2), mine], core_recv.at[0])
+    turn_raw(0)
+    for j in (1, 2, 3):
+        remote(
+            raw.at[0, :, lax.rem(x + j, 4)], raw_relay.at[0, :, :, xlane], raw_send, raw_recv.at[0], xdev(j)
+        )
+    turn_raw(1)
+    send_raw_z(1)
+    send_raw_z(3)
+    raw_relay[0, :, :, xlane] = raw[0, :, x]
+    raw_relay[1, :, :, zlane] = raw[1, z]
+
+    own_sums(2)
+    own_sums(3)
+    remote(lent_sum.at[later], got_sum.at[later], sum_send.at[1], sum_recv.at[1], {"c": oc})
+    wait_bytes(lead_x.at[pl.ds(0, 3)], sum_recv.at[2])
+    lead_z[z] = four(lead_x)
+    to_peers(lead_z, z, 3, zdev)
+    send_raw_z(2)
+    wait_bytes(lent_sum.at[later], sum_recv.at[1])
+    chip_sum[later] = own_sum[later] + got_sum[later]
+    scatter()
+    remote(swap.at[0, oc], swap.at[1, 0], rt_send.at[0], rt_recv.at[0], {"c": oc})
+    wait_bytes(lead_z.at[pl.ds(0, 3)], sum_recv.at[3])
+    total[lead] = four(lead_z)
     finish(lead)
-    first_hop(0)
-    for (first, n), _, _, me, dev, before, sem in plans:
-        at = pl.ds(first, n)
-        wait_bytes(stage_one.at[pl.ds(0, 3), at], sum_recv.at[before])
-        stage_two[me, at] = (stage_one[0, at] + stage_one[1, at]) + (stage_one[2, at] + stage_one[3, at])
-        for j in (1, 2, 3):
-            remote(stage_two.at[me, at], stage_two.at[me, at], sum_send.at[sem], sum_recv.at[sem], dev(j))
-    router_start()
-    for (first, n), _, _, _, _, _, sem in plans:
-        at = pl.ds(first, n)
-        wait_bytes(stage_two.at[pl.ds(0, 3), at], sum_recv.at[sem])
-        finish(at)
     wait_bytes(full.at[pl.ds(2, 6), mine], core_recv.at[1])
     first_hop(1)
+    first_hop(2)
+    across()
+    second_hop(0)
+    back()
+    router_start()
+    first_hop(3)
+    second_hop(1)
+    router_z()
+    for g, (first, n) in enumerate(LATER):
+        wait_bytes(total.at[pl.ds(first, 6)], sum_recv.at[8 + g])
+    finish(later)
     remote(scale, other, sc_send, sc_recv, {"c": oc})
-    router_z()
-    first_hop(2)
-    second_hop(0)
 
     def step(p, carry):
         first_hop(p)
         second_hop(p - LAG)
         return carry
 
-    step(3, 0)
     wait_bytes(full.at[pl.ds(8, 8), mine], core_recv.at[2])
     lax.fori_loop(4, 6, step, 0)
     router_y()
@@ -281,13 +335,14 @@
     wait_bytes(router.at[pl.ds(0, 4)], rt_send.at[4])
     for k, (first, n) in enumerate(CHUNKS):
         wait_bytes(full.at[pl.ds(first, n), mine], core_send.at[k])
-    wait_bytes(pair_sum.at[pl.ds(0, 7)], sum_send.at[0])
-    wait_bytes(lent_sum.at[rest], sum_send.at[1])
-    wait_bytes(stage_two.at[pl.ds(0, 3), lead], sum_send.at[2])
-    for (first, n), _, _, _, _, before, sem in plans:
-        wait_bytes(stage_one.at[pl.ds(0, 3), pl.ds(first, n)], sum_send.at[before])
-        wait_bytes(stage_two.at[pl.ds(0, 3), pl.ds(first, n)], sum_send.at[sem])
-    wait_bytes(turned.at[pl.ds(0, SLOTS * 3 // 4)], one_send)
+    wait_bytes(lent_sum.at[lead], sum_send.at[0])
+    wait_bytes(lent_sum.at[later], sum_send.at[1])
+    wait_bytes(lead_x.at[pl.ds(0, 3)], sum_send.at[2])
+    wait_bytes(lead_z.at[pl.ds(0, 3)], sum_send.at[3])
+    for k in range(6):
+        wait_bytes(total.at[pl.ds(0, 6)], sum_send.at[4 + k])
+    wait_bytes(raw.at[:, pl.ds(0, 3)], raw_send)
+    wait_bytes(turned.at[pl.ds(0, SLOTS - 2), pl.ds(0, 3)], one_send)
     wait_bytes(out.at[pl.ds(0, 42)], two_send)
     wait_bytes(out.at[pl.ds(0, 42)], two_recv)
 
@@ -328,12 +383,18 @@
             pltpu.VMEM((SLOTS, 64, 1024), F32),
             pltpu.VMEM((SLOTS, 4, 4, 64, 128), BF16),
             pltpu.VMEM((SLOTS, 4, 64, 512), BF16),
-            pltpu.VMEM(sums, F32),
-            pltpu.VMEM(sums, F32),
-            pltpu.VMEM(sums, F32),
-            pltpu.VMEM((8, 2, 1, 1024), F32),
-            pltpu.VMEM((4,) + sums, F32),
-            pltpu.VMEM((4,) + sums, F32),
+            pltpu.VMEM((2, 4, 4, 64, 128), F32),
+            pltpu.VMEM((2, 4, 64, 512), F32),
+            pltpu.VMEM((16, 64, 128), F32),
+            pltpu.VMEM(sums, F32),
+            pltpu.VMEM(sums, F32),
+            pltpu.VMEM(sums, F32),
+            pltpu.VMEM(sums, F32),
+            pltpu.VMEM((4, LEAD, 1, 1024), F32),
+            pltpu.VMEM((4, LEAD, 1, 1024), F32),
+            pltpu.VMEM((2, 4, 2, 1, 1024), F32),
+            pltpu.VMEM((2, 4, 2, 1, 1024), F32),
+            pltpu.VMEM(sums, F32),
             pltpu.VMEM(sums, F32),
             pltpu.VMEM(sums, F32),
             pltpu.VMEM(sums, F32),
@@ -341,7 +402,7 @@
             pltpu.VMEM((HALF, 128), BF16),
             pltpu.VMEM((16, 64), F32),
             pltpu.VMEM((1, 64), F32),
-            dma((2 * chunks + 2,)), dma((chunks,)), dma((chunks,)), dma((7,)), dma((7,)),
+            dma((2 * chunks + 2,)), dma((chunks,)), dma((chunks,)), dma((10,)), dma((10,)), dma, dma((2,)),
             dma, dma((SLOTS,)), dma, dma, dma, dma, dma((5,)), dma((5,)),
         ],
         compiler_params=pltpu.CompilerParams(

time: 92.8 us -> 92.7 us (level)
  no operation moved by 1% of the time
where the time goes in v3:
time: 92.7 us; the launch traced here: 92.6 us
  Pallas kernels  92 us (99%)
    pallas_call x1, Pallas kernels, body(): pl.pallas_call(kernel, out_shape=(pltpu.VMEM((48, 32, 2048), BF16), pltpu...  89.1 us
    pallas_call x1, Pallas kernels, body(): pl.pallas_call(writer, out_shape=(tensor,) * 3 + (column,) * 3 + (jax.Sha...  2.87 us

profile of v3, /device:TPU:1, one launch (start us, length us, event | category | flops | bytes accessed | tf_op | source)
XLA Modules:
  0.0 92.6 jit_solution(16573786119587704181)
XLA Ops:
  0.6 89.1 %shard_map.108 = (bf16[48,32,2048]{2,1,0:T(8,128)(2,1)S(1)}, f32[48,1,32]{2,1,0:T(1,128)S(1)}, bf16[8,8,2048]{2,1,0:T(8,128)(2,1)S(1)}) custom-call(f32[16,64,1024]{2,1,0:T(8,128)} %gate.1, f32[16,64,1024]{2,1,0:T(8,128)} %up.1, f32[16,64,1024]{2,1,0:T(8,128)} %bitcast.11, f32[16,64]{1,0:T(8,128)} %bitcast.12, f32[1,64]{1,0:T(1,128)} %bitcast.13), custom_call_target="tpu_custom_call" | custom-call | tf_op jit(solution)/shard_map/pallas_call | solution.py:372
  89.7 2.9 %shard_map.109 = (bf16[16,32,2048]{2,1,0:T(8,128)(2,1)}, bf16[16,32,2048]{2,1,0:T(8,128)(2,1)}, bf16[16,32,2048]{2,1,0:T(8,128)(2,1)}, f32[16,1,32]{2,1,0:T(1,12...) custom-call(bf16[48,32,2048]{2,1,0:T(8,128)(2,1)S(1)} %get-tuple-element.17.packed, ...), custom_call_target="tpu_custom_call" | custom-call | tf_op jit(solution)/shard_map/pallas_call | solution.py:425

commit v4 on v3

--- a/solution.py
+++ b/solution.py
@@ -70,7 +70,7 @@
         pltpu.make_async_copy(weight, weight_in, load_sem.at[2 * len(CHUNKS)]),
         pltpu.make_async_copy(gain, gain_in, load_sem.at[2 * len(CHUNKS) + 1]),
     ))
-    for pair in loads:
+    for pair in (loads[0], loads[1]):
         for copy in pair:
             copy.start()
 
@@ -90,18 +90,24 @@
         lax.fori_loop(first, first + n, one, 0)
 
     arrived(0)
+    for pair in loads[2:]:
+        for copy in pair:
+            copy.start()
     own_sums(0)
     arrived(1)
     own_sums(1)
-    arrived(2)
-    arrived(3)
     pl.semaphore_wait(barrier, len(peers))
 
     lead, later = pl.ds(0, LEAD), pl.ds(LEAD, SLOTS - LEAD)
     remote(lent_sum.at[lead], got_sum.at[lead], sum_send.at[0], sum_recv.at[0], {"c": oc})
-    for k, (first, n) in enumerate(CHUNKS):
+
+    def lend(k):
+        first, n = CHUNKS[k]
         at = pl.ds(first, n)
         remote(half.at[at], full.at[at, mine], core_send.at[k], core_recv.at[k], {"c": oc})
+
+    lend(0)
+    lend(1)
     for copy in loads[-1]:
         copy.wait()
     product = weight_in[...] * gain_in[...]
@@ -267,6 +273,10 @@
     raw_relay[0, :, :, xlane] = raw[0, :, x]
     raw_relay[1, :, :, zlane] = raw[1, z]
 
+    arrived(2)
+    lend(2)
+    arrived(3)
+    lend(3)
     own_sums(2)
     own_sums(3)
     remote(lent_sum.at[later], got_sum.at[later], sum_send.at[1], sum_recv.at[1], {"c": oc})

time: 92.7 us -> 90.5 us (0.976)
  Pallas kernels: 92 us -> 89.7 us
    pallas_call x1, Pallas kernels: 89.1 us -> 86.9 us  [body(): pl.pallas_call(kernel, out_shape=(pltpu.VMEM((48, 32, 2048), BF16), pltpu...]
where the time goes in v4:
time: 90.5 us; the launch traced here: 90.4 us
  Pallas kernels  89.7 us (99%)
    pallas_call x1, Pallas kernels, body(): pl.pallas_call(kernel, out_shape=(pltpu.VMEM((48, 32, 2048), BF16), pltpu...  86.9 us
    pallas_call x1, Pallas kernels, body(): pl.pallas_call(writer, out_shape=(tensor,) * 3 + (column,) * 3 + (jax.Sha...  2.87 us

profile of v4, /device:TPU:1, one launch (start us, length us, event | category | flops | bytes accessed | tf_op | source)
XLA Modules:
  0.0 90.4 jit_solution(6543023958110685597)
XLA Ops:
  0.6 86.9 %shard_map.108 = (bf16[48,32,2048]{2,1,0:T(8,128)(2,1)S(1)}, f32[48,1,32]{2,1,0:T(1,128)S(1)}, bf16[8,8,2048]{2,1,0:T(8,128)(2,1)S(1)}) custom-call(f32[16,64,1024]{2,1,0:T(8,128)} %gate.1, f32[16,64,1024]{2,1,0:T(8,128)} %up.1, f32[16,64,1024]{2,1,0:T(8,128)} %bitcast.11, f32[16,64]{1,0:T(8,128)} %bitcast.12, f32[1,64]{1,0:T(1,128)} %bitcast.13), custom_call_target="tpu_custom_call" | custom-call | tf_op jit(solution)/shard_map/pallas_call | solution.py:382
  87.5 2.9 %shard_map.109 = (bf16[16,32,2048]{2,1,0:T(8,128)(2,1)}, bf16[16,32,2048]{2,1,0:T(8,128)(2,1)}, bf16[16,32,2048]{2,1,0:T(8,128)(2,1)}, f32[16,1,32]{2,1,0:T(1,12...) custom-call(bf16[48,32,2048]{2,1,0:T(8,128)(2,1)S(1)} %get-tuple-element.17.packed, ...), custom_call_target="tpu_custom_call" | custom-call | tf_op jit(solution)/shard_map/pallas_call | solution.py:435
